TPU v7x, 32 devices: a whole 2x2x4 slice. The times are simulated.
32 devices in a mesh: dp: 8 (over z, y), group: 4 (over x, core).
Axes of the slice: x: 2, y: 2, z: 4, core: 2. Of those that a mesh axis runs over, the one named last changes fastest.
Arguments:
- rewards: bfloat16 [8192, 4096], P(('dp', 'group')), may hold values from -6 to 6
- values: bfloat16 [8192, 4096], P(('dp', 'group')), may hold values from -6 to 6
- lengths: int32 [8192], P(('dp', 'group')), may hold values from 1 to 4096
- decay_rate: float32 [8192], P(('dp', 'group')), may hold values from 3.8146973e-06 to 0.03125
- piece_dest: int32 [8, 8], P('dp'), may hold values from 0 to 7, each once within a row
- row_perm: int32 [64, 128], P(('dp', 'group')), may hold values from 0 to 127, each once within a row
- minibatch: int32 [8192], P(('dp', 'group')), may hold values from 0 to 63
Outputs:
- white_rewards: bfloat16 [8192, 4096], P(('dp', 'group'))
- white_advantage: bfloat16 [8192, 4096], P(('dp', 'group'))
Inputs may be any that keep to these rules, and one draw needn't show every extreme that they name: Each row of piece_dest names every index of dp once. Each row of row_perm names every number below 128 once.
All inputs are finite; a program needn't handle non-finite values.
Results may differ from a plain program's by a relative error of at most 0.0049.
Values may be sent and summed in bfloat16 or wider, within the bound.
A program may use at most 64 MiB of HBM per device.

v0:
```python
import jax
import jax.numpy as jnp
from jax import lax
from jax.sharding import PartitionSpec as P

MINIBATCHES = 64
HIGHEST = lax.Precision.HIGHEST


def discounted(rewards, values, lengths, decay_rate):
    rows_here, span = rewards.shape
    block = min(128, span)
    blocks_here = span // block
    position = jnp.arange(span, dtype=jnp.int32)
    is_valid = position[None, :] < lengths[:, None]
    next_valid = position[None, :] + 1 < lengths[:, None]
    per_step = jnp.exp(-decay_rate)
    value_f = values.astype(jnp.float32)
    value_next = jnp.concatenate([value_f[:, 1:], jnp.zeros((rows_here, 1), jnp.float32)], axis=1)
    td_error = (
        rewards.astype(jnp.float32)
        + per_step[:, None] * jnp.where(next_valid, value_next, 0.0)
        - value_f
    )
    td_error = jnp.where(is_valid, td_error, 0.0).reshape(rows_here, blocks_here, block)
    offset = jnp.arange(block, dtype=jnp.float32)
    lower_scale = jnp.exp(-decay_rate[:, None] * offset[None, :])
    upper_scale = jnp.exp(decay_rate[:, None] * offset[None, :])
    triangle = (offset[:, None] >= offset[None, :]).astype(jnp.float32)
    scaled = td_error * lower_scale[:, None, :]
    summed = jnp.einsum("rjk,kt->rjt", scaled, triangle, precision=HIGHEST)
    local_part = summed * upper_scale[:, None, :]
    heads = local_part[:, :, 0]
    block_step = jnp.exp(-decay_rate * block)

    def carry_step(carry, head):
        fresh = head + block_step * carry
        return (fresh, fresh)

    final_carry, starts = lax.scan(carry_step, jnp.zeros_like(decay_rate), heads.T, reverse=True)
    next_heads = jnp.concatenate([starts[1:].T, jnp.zeros((rows_here, 1), jnp.float32)], axis=1)
    reach = jnp.exp(-decay_rate[:, None] * (block - offset[None, :]))
    total = local_part + reach[:, None, :] * next_heads[:, :, None]
    return jnp.where(is_valid, total.reshape(rows_here, span), 0.0).astype(jnp.bfloat16)


def by_target(array, piece_dest):
    peers = piece_dest.shape[1]
    target = piece_dest[0]
    slots = jnp.arange(peers, dtype=jnp.int32)
    source_slot = jnp.sum(jnp.where(target[None, :] == slots[:, None], slots[None, :], 0), axis=1)
    pieces = array.reshape((peers, array.shape[0] // peers) + array.shape[1:])
    return jnp.take(pieces, source_slot, axis=0).reshape(array.shape)


def reorder(received, row_perm):
    blocks_here, block = row_perm.shape
    chooser = (row_perm[:, :, None] == jnp.arange(block, dtype=jnp.int32)[None, None, :]).astype(
        jnp.bfloat16
    )

    def permute_one(member):
        shaped = member.reshape(blocks_here, block, member.shape[-1])
        mixed = jnp.einsum("bim,bmc->bic", chooser, shaped, preferred_element_type=jnp.float32)
        return mixed.astype(jnp.bfloat16).reshape(member.shape)

    return tuple((permute_one(member) for member in received))


def whiten(rewards, advantage, lengths, minibatch):
    rows_here, span = rewards.shape
    position = jnp.arange(span, dtype=jnp.int32)
    is_valid = position[None, :] < lengths[:, None]
    counted = lengths.astype(jnp.float32)
    reward_f = jnp.where(is_valid, rewards.astype(jnp.float32), 0.0)
    advantage_f = jnp.where(is_valid, advantage.astype(jnp.float32), 0.0)
    member = (minibatch[:, None] == jnp.arange(MINIBATCHES, dtype=jnp.int32)[None, :]).astype(
        jnp.float32
    )
    row_terms = jnp.stack(
        [
            counted,
            jnp.sum(reward_f, axis=1),
            jnp.sum(advantage_f, axis=1),
            jnp.sum(reward_f * reward_f, axis=1),
            jnp.sum(advantage_f * advantage_f, axis=1),
        ],
        axis=1,
    )
    totals = lax.psum(jnp.dot(member.T, row_terms, precision=HIGHEST), ("dp", "group"))
    count = jnp.maximum(totals[:, 0], 1.0)
    means = totals[:, 1:3] / count[:, None]
    spreads = totals[:, 3:5] / count[:, None] - means * means
    row_means = jnp.dot(member, means, precision=HIGHEST)
    row_scale = jnp.dot(member, lax.rsqrt(spreads + 1e-05), precision=HIGHEST)
    white_rewards = jnp.where(is_valid, (reward_f - row_means[:, 0:1]) * row_scale[:, 0:1], 0.0)
    white_advantage = jnp.where(
        is_valid, (advantage_f - row_means[:, 1:2]) * row_scale[:, 1:2], 0.0
    )
    return (white_rewards.astype(jnp.bfloat16), white_advantage.astype(jnp.bfloat16))


def local(rewards, values, lengths, decay_rate, piece_dest, row_perm, minibatch):
    blocks_here, block = row_perm.shape
    new_order = (jnp.arange(blocks_here, dtype=jnp.int32)[:, None] * block + row_perm).reshape(-1)
    per_row = jnp.stack([lengths.astype(jnp.float32), decay_rate], axis=1)
    moved_terms = lax.all_to_all(
        by_target(per_row, piece_dest), "dp", split_axis=0, concat_axis=0, tiled=True
    )
    moved_terms = jnp.take(moved_terms, new_order, axis=0)
    lengths_here = moved_terms[:, 0].astype(jnp.int32)
    rate_here = moved_terms[:, 1]
    moved_rewards, moved_second = reorder(
        (
            lax.all_to_all(
                by_target(rewards, piece_dest), "dp", split_axis=0, concat_axis=0, tiled=True
            ),
            lax.all_to_all(
                by_target(values, piece_dest), "dp", split_axis=0, concat_axis=0, tiled=True
            ),
        ),
        row_perm,
    )
    advantage = discounted(moved_rewards, moved_second, lengths_here, rate_here)
    return whiten(moved_rewards, advantage, lengths_here, minibatch)


def solution(mesh):
    return jax.shard_map(
        local,
        mesh=mesh,
        in_specs=(
            P(("dp", "group"), None),
            P(("dp", "group"), None),
            P(("dp", "group")),
            P(("dp", "group")),
            P("dp", None),
            P(("dp", "group"), None),
            P(("dp", "group")),
        ),
        out_specs=(P(("dp", "group"), None), P(("dp", "group"), None)),
        check_vma=False,
    )
```

profile of v0, /device:TPU:10, one launch (start us, length us, event | category | flops | bytes accessed | tf_op | source)
XLA Modules:
  0.0 195.4 jit_solution(8454684337441469848)
XLA Ops:
  0.6 0.0 copy-start
  0.6 0.9 select_reduce_fusion
  1.6 0.7 convert_element_type.58
  2.3 0.1 stack.25
  2.4 0.8 stack.26
  3.1 0.6 gather_fusion
  3.7 0.7 broadcast_select_fusion.3
  4.4 6.3 %all-to-all-start = ((f32[8,32,2]{1,2,0:T(2,128)}), f32[8,32,2]{1,2,0:T(2,128)S(1)}, u32[]{:S(2)}, u32[]{:S(2)}) async-start(f32[8,32,2]{1,2,0:T(2,128)} %broadcast_select_fusion.3), calls=%async_computation | async-start | bytes 16384 | tf_op jit(solution)/shard_map/all_to_all | solution.py:107
  10.7 0.0 copy-done
  10.7 2.0 %gather_fusion.2 = bf16[8,32,4096]{2,1,0:T(8,128)(2,1)} fusion(bf16[8,32,4096]{2,1,0:T(8,128)(2,1)S(1)} %bitcast.76, s32[1024]{0:T(1024)S(1)} %pad_clamp_fusion), kind=kCustom, calls=%fused_computation.clone | custom fusion | bytes 4194336 | tf_op jit(solution)/shard_map/jit(_take)/gather | solution.py:53
  12.7 3.6 %gather_fusion.3 = bf16[8,32,4096]{2,1,0:T(8,128)(2,1)} fusion(bf16[8,32,4096]{2,1,0:T(8,128)(2,1)} %bitcast.80, s32[1024]{0:T(1024)S(1)} %pad_clamp_fusion), kind=kCustom, calls=%fused_computation.1.clone | custom fusion | bytes 4194336 | tf_op jit(solution)/shard_map/jit(_take)/gather | solution.py:53
  16.3 4.7 %broadcast_select_fusion = (bf16[8,32,4096]{2,1,0:T(8,128)(2,1)}, bf16[8,32,4096]{2,1,0:T(8,128)(2,1)}) fusion(bf16[8,32,4096]{2,1,0:T(8,128)(2,1)} %gather_fusion.3, pred[8]{0:T(512)(128)(4,1)S(1)} %compare_and_fusion, bf16[8,32,4096]{2,1,0:T(8,128)(2,1)} %gather_fusion.2), kind=kLoop, calls=%fused_computation.37 | loop fusion | flops 2097152 | bytes 8388616 | tf_op jit(solution)/shard_map/jit(_take)/select_n | solution.py:53
  20.9 0.0 all-to-all-done
  20.9 53.1 %all_to_all.21 = bf16[8,32,4096]{2,1,0:T(8,128)(2,1)} all-to-all(bf16[8,32,4096]{2,1,0:T(8,128)(2,1)} %get-tuple-element.154), channel_id=1, replica_groups=mesh['dp'=8,'group'=4] {'dp'}, dimensions={0} | all-to-all | bytes 4194304 | tf_op jit(solution)/shard_map/all_to_all | solution.py:118
  74.0 5.2 %all-to-all-start.1 = ((bf16[8,32,4096]{2,1,0:T(8,128)(2,1)}), bf16[8,32,4096]{2,1,0:T(8,128)(2,1)}, u32[]{:S(2)}, u32[]{:S(2)}) async-start(bf16[8,32,4096]{2,1,0:T(8,128)(2,1)} %get-tuple-element.155), calls=%async_computation.1 | async-start | bytes 4194304 | tf_op jit(solution)/shard_map/all_to_all | solution.py:115
  79.2 0.0 copy-done.6
  79.2 0.1 compare_and_fusion.1
  79.3 0.1 copy.56
  79.4 0.7 gather_fusion.1
  80.2 0.1 broadcast_select_fusion.2
  80.3 0.3 fusion.21
  80.5 0.1 multiply_exponential_fusion
  80.6 0.1 copy.52
  80.7 0.1 copy.54
  80.8 0.1 fusion.20
  81.0 2.3 %convolution_convert_fusion = bf16[2,128,4096]{2,1,0:T(8,128)(2,1)S(1)} fusion(bf16[2,128,4096]{2,1,0:T(8,128)(2,1)} %bitcast.78, s32[2,128]{1,0:T(2,128)S(1)} %copy-done.6), kind=kOutput, calls=%fused_computation.9 | convolution fusion | flops 269516800 | bytes 4195328 | tf_op jit(solution)/shard_map/bim,bmc->bic/dot_general | solution.py:64
  83.3 0.0 copy-start.1
  83.3 1.3 copy-done.1
  84.6 0.6 bitcast_convert_fusion
  85.3 3.1 %slice.58 = f32[256,4095]{1,0:T(8,128)} slice(f32[256,4096]{1,0:T(8,128)S(1)} %bitcast_convert_fusion), slice={[0:256], [1:4096]} | slice | bytes 8386560 | tf_op jit(solution)/shard_map/slice | solution.py:19
  88.4 34.9 %all-to-all-done.1 = bf16[8,32,4096]{2,1,0:T(8,128)(2,1)} async-done(((bf16[8,32,4096]{2,1,0:T(8,128)(2,1)}), bf16[8,32,4096]{2,1,0:T(8,128)(2,1)}, u32[]{:S(2)}, u32[]{:S(2)}) %all-to-all-start.1) | async-done | bytes 2097184 | tf_op jit(solution)/shard_map/all_to_all | solution.py:115
  123.3 3.0 %multiply_reduce_fusion.1 = (f32[2,128]{1,0:T(2,128)S(1)}, f32[2,128]{1,0:T(2,128)S(1)}, f32[2,128,4096]{2,1,0:T(8,128)S(1)}) fusion(s32[2,128]{1,0:T(2,128)S(1)} %bitcast.84, bf16[2,128,4096]{2,1,0:T(8,128)(2,1)} %bitcast.10, s32[2,128]{1,0:T(2,128)S(1)} %copy-done.6), kind=kOutput, calls=%fused_computation.27 | convolution fusion | flops 275807744 | bytes 6295552 | tf_op jit(solution)/shard_map/bim,bmc->bic/dot_general | solution.py:64
  126.3 0.0 copy-start.4
  126.3 0.0 copy-done.2
  126.4 0.4 copy-done.5
  126.8 1.8 fusion.10
  128.6 0.0 copy-done.4
  128.6 2.9 %fusion.14 = f32[256,32,128]{0,2,1:T(8,128)S(1)} fusion(f32[256,128]{0,1:T(8,128)S(1)} %get-tuple-element.157, f32[256,128]{1,0:T(8,128)S(1)} %copy.52, f32[256,4096]{1,0:T(8,128)S(1)} %fusion.10), kind=kOutput, calls=%fused_computation.34 | convolution fusion | flops 1612726272 | bytes 8650752 | tf_op jit(solution)/shard_map/rjk,kt->rjt/dot_general | solution.py:31
  131.5 2.0 %copy-done.3 = f32[256,32,128]{0,2,1:T(8,128)} copy-done((f32[256,32,128]{0,2,1:T(8,128)}, f32[256,32,128]{0,2,1:T(8,128)S(1)}, u32[]{:S(2)}) %copy-start.3) | copy-done | bytes 4194328
  133.5 3.3 %while.17 = (s32[]{:T(128)}, f32[256]{0:T(256)S(1)}, f32[32,256]{1,0:T(8,128)S(1)}, f32[32,256]{1,0:T(8,128)S(1)}, f32[256]{0:T(256)S(1)}, /*index=5*/s32[]{:T(128)}, s32[]{:T(128)}, s32[]{:T(128)}) while((s32[]{:T(128)}, f32[256]{0:T(256)S(1)}, f32[32,256]{1,0:T(8,128)S(1)}, f32[32,256]{1,0:T(8,128)S(1)}, f32[256]{0:T(256)S(1)}, ...), condition=%wide.region_3.5_spmd.clone, body=%wide.region_2.4_spmd.clone.sunk | while | flops 772 | bytes 8307 | solution.py:40
  136.8 5.0 %multiply_reduce_fusion = (f32[256]{0:T(256)S(1)}, f32[256]{0:T(256)S(1)}, bf16[256,32,128]{0,2,1:T(8,128)(2,1)}) fusion(s32[256]{0:T(256)S(1)} %fusion.20, s32[32,128]{1,0:T(8,128)S(1)} %multiply_add_fusion.1, f32[256,32,128]{0,2,1:T(8,128)} %copy-done.3, f32[256,32]{0,1:T(8,128)S(1)} %concatenate.8, f32[256,128]{0,1:T(8,128)S(1)} %get-tuple-element.152), kind=kLoop, calls=%fused_computation.26 | loop fusion | flops 10485248 | bytes 6474752 | tf_op jit(solution)/shard_map/reduce_sum | solution.py:86
  141.9 0.2 fusion.18
  142.1 42.8 %psum.7 = f32[64,5]{0,1:T(8,128)S(1)} all-reduce(f32[64,5]{0,1:T(8,128)S(1)} %fusion.18), channel_id=1, replica_groups=mesh['dp'=8,'group'=4] {'dp','group'}, use_global_device_ids=true, to_apply=%region_7.9 | all-reduce | flops 320 | bytes 2560 | tf_op jit(solution)/shard_map/psum | solution.py:90
  184.9 0.2 fusion.17
  185.1 0.3 fusion.16
  185.3 0.1 fusion.37
  185.4 4.1 %copy.55 = bf16[256,4096]{1,0:T(8,128)(2,1)} copy(bf16[256,4096]{0,1:T(8,128)(2,1)} %bitcast.79) | data formatting | bytes 4194304 | tf_op jit(solution)/shard_map/reshape | solution.py:44
  189.5 5.9 %select_convert_fusion = (bf16[256,4096]{1,0:T(8,128)(2,1)}, bf16[256,4096]{1,0:T(8,128)(2,1)}) fusion(bf16[256,4096]{1,0:T(8,128)(2,1)} %copy.55, f32[256]{0:T(256)S(1)} %bitcast.89, f32[256]{0:T(256)S(1)} %bitcast.87, s32[256]{0:T(256)S(1)} %fusion.20, f32[256]{0:T(256)S(1)} %bitcast.90, f32[256]{0:T(256)S(1)} %bitcast.88, f32[2,128,4096]{2,1,0:T(8,128)} %copy-done.4), kind=kLoop, calls=%fused_computation.24 | loop fusion | flops 13631488 | bytes 10490880 | tf_op jit(solution)/shard_map/convert_element_type | solution.py:100
  (124 shorter events, 2.3 us)
Async XLA Ops:
  0.6 10.0 %copy-start = (bf16[256,4096]{1,0:T(8,128)(2,1)S(1)}, bf16[256,4096]{1,0:T(8,128)(2,1)}, u32[]{:S(2)}) copy-start(bf16[256,4096]{1,0:T(8,128)(2,1)} %param.11) | copy-start | bytes 6291460
  4.4 16.6 %all-to-all-start = ((f32[8,32,2]{1,2,0:T(2,128)}), f32[8,32,2]{1,2,0:T(2,128)S(1)}, u32[]{:S(2)}, u32[]{:S(2)}) async-start(f32[8,32,2]{1,2,0:T(2,128)} %broadcast_select_fusion.3), calls=%async_computation | async-start | bytes 16384 | tf_op jit(solution)/shard_map/all_to_all | solution.py:107
  20.9 58.2 %copy-start.6 = (s32[2,128]{1,0:T(2,128)S(1)}, s32[2,128]{1,0:T(2,128)}, u32[]{:S(2)}) copy-start(s32[2,128]{1,0:T(2,128)} %param.16) | copy-start | bytes 3076
  74.0 49.3 %all-to-all-start.1 = ((bf16[8,32,4096]{2,1,0:T(8,128)(2,1)}), bf16[8,32,4096]{2,1,0:T(8,128)(2,1)}, u32[]{:S(2)}, u32[]{:S(2)}) async-start(bf16[8,32,4096]{2,1,0:T(8,128)(2,1)} %get-tuple-element.155), calls=%async_computation.1 | async-start | bytes 4194304 | tf_op jit(solution)/shard_map/all_to_all | solution.py:115
  83.3 1.3 copy-start.1
  123.3 3.0 %copy-start.2 = (bf16[2,128,4096]{2,1,0:T(8,128)(2,1)S(1)}, bf16[2,128,4096]{2,1,0:T(8,128)(2,1)}, u32[]{:S(2)}) copy-start(bf16[2,128,4096]{2,1,0:T(8,128)(2,1)} %copy-done.1) | copy-start | bytes 6291460
  123.3 3.5 %copy-start.5 = (f32[256,4095]{1,0:T(8,128)S(1)}, f32[256,4095]{1,0:T(8,128)}, u32[]{:S(2)}) copy-start(f32[256,4095]{1,0:T(8,128)} %slice.58) | copy-start | bytes 12579844
  126.3 2.2 %copy-start.4 = (f32[2,128,4096]{2,1,0:T(8,128)}, f32[2,128,4096]{2,1,0:T(8,128)S(1)}, u32[]{:S(2)}) copy-start(f32[2,128,4096]{2,1,0:T(8,128)S(1)} %get-tuple-element.156) | copy-start | bytes 12582916
  131.5 2.0 %copy-start.3 = (f32[256,32,128]{0,2,1:T(8,128)}, f32[256,32,128]{0,2,1:T(8,128)S(1)}, u32[]{:S(2)}) copy-start(f32[256,32,128]{0,2,1:T(8,128)S(1)} %fusion.14) | copy-start | bytes 12582916
  133.4 8.4 %copy-start.7 = (s32[256]{0:T(256)S(1)}, s32[256]{0:T(256)}, u32[]{:S(2)}) copy-start(s32[256]{0:T(256)} %param.17) | copy-start | bytes 3076
where the time goes:
time: 196 us; the launch traced here: 195 us
  blocking collectives  95.8 us (49%)
  waiting for transfers between devices  34.9 us (18%)
  other arithmetic  21.5 us (11%)
  local copies, waits for them, and re-layouts  20.8 us (11%)
  starting transfers between devices  11.4 us (6%)
  matrix products  8.91 us (5%)
    all_to_all x1, blocking collectives, local(): lax.all_to_all(by_target(values, piece_dest), 'dp', split_axis=0, concat_...  53.1 us
    psum x1, blocking collectives, whiten(): lax.psum(jnp.dot(member.T, row_terms, precision=HIGHEST), ('dp', 'group'))  42.8 us
    all_to_all x1, waiting for transfers between devices, local(): lax.all_to_all(by_target(rewards, piece_dest), 'dp', split_axis=0, concat...  34.9 us
    all_to_all x1, starting transfers between devices, local(): lax.all_to_all(by_target(per_row, piece_dest), 'dp', split_axis=0, concat...  6.28 us
    gather x3, local copies, waits for them, and re-layouts, by_target(): return jnp.take(pieces, source_slot, axis=0).reshape(array.shape)  6.16 us
    convert_element_type x1, other arithmetic, whiten(): white_advantage.astype(jnp.bfloat16)  5.93 us
    dot_general x2, matrix products, permute_one(): jnp.einsum('bim,bmc->bic', chooser, shaped, preferred_element_type=jnp.fl...  5.36 us
    select_n x4, other arithmetic, by_target(): return jnp.take(pieces, source_slot, axis=0).reshape(array.shape)  5.35 us
  transfers between devices with their start and end apart: 2, of which 1 were waited for; matrix products, arithmetic and copies ran while one was open for 9% of the time, Pallas kernels for 0%

commit v1 on v0

--- a/solution.py
+++ b/solution.py
@@ -87,7 +87,7 @@
         ],
         axis=1,
     )
-    totals = lax.psum(jnp.dot(member.T, row_terms, precision=HIGHEST), ("dp", "group"))
+    totals = lax.psum(lax.psum(jnp.dot(member.T, row_terms, precision=HIGHEST), "group"), "dp")
     count = jnp.maximum(totals[:, 0], 1.0)
     means = totals[:, 1:3] / count[:, None]
     spreads = totals[:, 3:5] / count[:, None] - means * means

time: 196 us -> 184 us (0.939)
  the two profiles are of different devices: /device:TPU:10 before, /device:TPU:0 now
where the time goes in v1:
time: 184 us; the launch traced here: 183 us
  blocking collectives  80.3 us (44%)
  waiting for transfers between devices  38 us (21%)
  other arithmetic  21.5 us (12%)
  local copies, waits for them, and re-layouts  20.8 us (11%)
  starting transfers between devices  11.7 us (6%)
  matrix products  8.91 us (5%)
    all_to_all x1, blocking collectives, local(): lax.all_to_all(by_target(values, piece_dest), 'dp', split_axis=0, concat_...  54 us
    all_to_all x1, waiting for transfers between devices, local(): lax.all_to_all(by_target(rewards, piece_dest), 'dp', split_axis=0, concat...  38 us
    psum x1, blocking collectives, whiten(): lax.psum(lax.psum(jnp.dot(member.T, row_terms, precision=HIGHEST), 'group...  20.7 us
    all_to_all x1, starting transfers between devices, local(): lax.all_to_all(by_target(per_row, piece_dest), 'dp', split_axis=0, concat...  7.31 us
    gather x3, local copies, waits for them, and re-layouts, by_target(): return jnp.take(pieces, source_slot, axis=0).reshape(array.shape)  6.16 us
    convert_element_type x1, other arithmetic, whiten(): white_advantage.astype(jnp.bfloat16)  5.93 us
    psum x1, blocking collectives, whiten(): lax.psum(jnp.dot(member.T, row_terms, precision=HIGHEST), 'group')  5.65 us
    dot_general x2, matrix products, permute_one(): jnp.einsum('bim,bmc->bic', chooser, shaped, preferred_element_type=jnp.fl...  5.35 us
  transfers between devices with their start and end apart: 2, of which 1 were waited for; matrix products, arithmetic and copies ran while one was open for 10% of the time, Pallas kernels for 0%

profile of v1, /device:TPU:0, one launch (start us, length us, event | category | flops | bytes accessed | tf_op | source)
XLA Modules:
  0.0 183.2 jit_solution(14429782176399896438)
XLA Ops:
  0.6 0.0 copy-start
  0.6 0.9 select_reduce_fusion
  1.6 0.7 convert_element_type.58
  2.3 0.1 stack.25
  2.4 0.8 stack.26
  3.1 0.6 gather_fusion
  3.7 0.7 broadcast_select_fusion.3
  4.4 7.3 %all-to-all-start = ((f32[8,32,2]{1,2,0:T(2,128)}), f32[8,32,2]{1,2,0:T(2,128)S(1)}, u32[]{:S(2)}, u32[]{:S(2)}) async-start(f32[8,32,2]{1,2,0:T(2,128)} %broadcast_select_fusion.3), calls=%async_computation | async-start | bytes 16384 | tf_op jit(solution)/shard_map/all_to_all | solution.py:107
  11.7 0.0 copy-done
  11.7 2.0 %gather_fusion.2 = bf16[8,32,4096]{2,1,0:T(8,128)(2,1)} fusion(bf16[8,32,4096]{2,1,0:T(8,128)(2,1)S(1)} %bitcast.76, s32[1024]{0:T(1024)S(1)} %pad_clamp_fusion), kind=kCustom, calls=%fused_computation.clone | custom fusion | bytes 4194336 | tf_op jit(solution)/shard_map/jit(_take)/gather | solution.py:53
  13.7 3.6 %gather_fusion.3 = bf16[8,32,4096]{2,1,0:T(8,128)(2,1)} fusion(bf16[8,32,4096]{2,1,0:T(8,128)(2,1)} %bitcast.80, s32[1024]{0:T(1024)S(1)} %pad_clamp_fusion), kind=kCustom, calls=%fused_computation.1.clone | custom fusion | bytes 4194336 | tf_op jit(solution)/shard_map/jit(_take)/gather | solution.py:53
  17.3 4.7 %broadcast_select_fusion = (bf16[8,32,4096]{2,1,0:T(8,128)(2,1)}, bf16[8,32,4096]{2,1,0:T(8,128)(2,1)}) fusion(bf16[8,32,4096]{2,1,0:T(8,128)(2,1)} %gather_fusion.3, pred[8]{0:T(512)(128)(4,1)S(1)} %compare_and_fusion, bf16[8,32,4096]{2,1,0:T(8,128)(2,1)} %gather_fusion.2), kind=kLoop, calls=%fused_computation.37 | loop fusion | flops 2097152 | bytes 8388616 | tf_op jit(solution)/shard_map/jit(_take)/select_n | solution.py:53
  22.0 0.0 all-to-all-done
  22.0 54.0 %all_to_all.21 = bf16[8,32,4096]{2,1,0:T(8,128)(2,1)} all-to-all(bf16[8,32,4096]{2,1,0:T(8,128)(2,1)} %get-tuple-element.154), channel_id=1, replica_groups=mesh['dp'=8,'group'=4] {'dp'}, dimensions={0} | all-to-all | bytes 4194304 | tf_op jit(solution)/shard_map/all_to_all | solution.py:118
  76.0 4.3 %all-to-all-start.1 = ((bf16[8,32,4096]{2,1,0:T(8,128)(2,1)}), bf16[8,32,4096]{2,1,0:T(8,128)(2,1)}, u32[]{:S(2)}, u32[]{:S(2)}) async-start(bf16[8,32,4096]{2,1,0:T(8,128)(2,1)} %get-tuple-element.155), calls=%async_computation.1 | async-start | bytes 4194304 | tf_op jit(solution)/shard_map/all_to_all | solution.py:115
  80.4 0.0 copy-done.6
  80.4 0.1 compare_and_fusion.1
  80.5 0.1 copy.56
  80.6 0.7 gather_fusion.1
  81.3 0.1 broadcast_select_fusion.2
  81.4 0.3 fusion.21
  81.7 0.1 multiply_exponential_fusion
  81.8 0.1 copy.52
  81.9 0.1 copy.54
  82.0 0.1 fusion.20
  82.1 2.3 %convolution_convert_fusion = bf16[2,128,4096]{2,1,0:T(8,128)(2,1)S(1)} fusion(bf16[2,128,4096]{2,1,0:T(8,128)(2,1)} %bitcast.78, s32[2,128]{1,0:T(2,128)S(1)} %copy-done.6), kind=kOutput, calls=%fused_computation.9 | convolution fusion | flops 269516800 | bytes 4195328 | tf_op jit(solution)/shard_map/bim,bmc->bic/dot_general | solution.py:64
  84.5 0.0 copy-start.1
  84.5 1.3 copy-done.1
  85.8 0.6 bitcast_convert_fusion
  86.4 3.1 %slice.58 = f32[256,4095]{1,0:T(8,128)} slice(f32[256,4096]{1,0:T(8,128)S(1)} %bitcast_convert_fusion), slice={[0:256], [1:4096]} | slice | bytes 8386560 | tf_op jit(solution)/shard_map/slice | solution.py:19
  89.5 38.0 %all-to-all-done.1 = bf16[8,32,4096]{2,1,0:T(8,128)(2,1)} async-done(((bf16[8,32,4096]{2,1,0:T(8,128)(2,1)}), bf16[8,32,4096]{2,1,0:T(8,128)(2,1)}, u32[]{:S(2)}, u32[]{:S(2)}) %all-to-all-start.1) | async-done | bytes 2097184 | tf_op jit(solution)/shard_map/all_to_all | solution.py:115
  127.6 3.0 %multiply_reduce_fusion.1 = (f32[2,128]{1,0:T(2,128)S(1)}, f32[2,128]{1,0:T(2,128)S(1)}, f32[2,128,4096]{2,1,0:T(8,128)S(1)}) fusion(s32[2,128]{1,0:T(2,128)S(1)} %bitcast.84, bf16[2,128,4096]{2,1,0:T(8,128)(2,1)} %bitcast.10, s32[2,128]{1,0:T(2,128)S(1)} %copy-done.6), kind=kOutput, calls=%fused_computation.27 | convolution fusion | flops 275807744 | bytes 6295552 | tf_op jit(solution)/shard_map/bim,bmc->bic/dot_general | solution.py:64
  130.6 0.0 copy-start.4
  130.6 0.0 copy-done.2
  130.6 0.4 copy-done.5
  131.0 1.8 fusion.10
  132.8 2.9 %fusion.14 = f32[256,32,128]{0,2,1:T(8,128)S(1)} fusion(f32[256,128]{0,1:T(8,128)S(1)} %get-tuple-element.157, f32[256,128]{1,0:T(8,128)S(1)} %copy.52, f32[256,4096]{1,0:T(8,128)S(1)} %fusion.10), kind=kOutput, calls=%fused_computation.34 | convolution fusion | flops 1612726272 | bytes 8650752 | tf_op jit(solution)/shard_map/rjk,kt->rjt/dot_general | solution.py:31
  135.7 2.0 %copy-done.3 = f32[256,32,128]{0,2,1:T(8,128)} copy-done((f32[256,32,128]{0,2,1:T(8,128)}, f32[256,32,128]{0,2,1:T(8,128)S(1)}, u32[]{:S(2)}) %copy-start.3) | copy-done | bytes 4194328
  137.7 3.3 %while.17 = (s32[]{:T(128)}, f32[256]{0:T(256)S(1)}, f32[32,256]{1,0:T(8,128)S(1)}, f32[32,256]{1,0:T(8,128)S(1)}, f32[256]{0:T(256)S(1)}, /*index=5*/s32[]{:T(128)}, s32[]{:T(128)}, s32[]{:T(128)}) while((s32[]{:T(128)}, f32[256]{0:T(256)S(1)}, f32[32,256]{1,0:T(8,128)S(1)}, f32[32,256]{1,0:T(8,128)S(1)}, f32[256]{0:T(256)S(1)}, ...), condition=%wide.region_3.5_spmd.clone, body=%wide.region_2.4_spmd.clone.sunk | while | flops 772 | bytes 8307 | solution.py:40
  141.0 5.0 %multiply_reduce_fusion = (f32[256]{0:T(256)S(1)}, f32[256]{0:T(256)S(1)}, bf16[256,32,128]{0,2,1:T(8,128)(2,1)}) fusion(s32[256]{0:T(256)S(1)} %fusion.20, s32[32,128]{1,0:T(8,128)S(1)} %multiply_add_fusion.1, f32[256,32,128]{0,2,1:T(8,128)} %copy-done.3, f32[256,32]{0,1:T(8,128)S(1)} %concatenate.8, f32[256,128]{0,1:T(8,128)S(1)} %get-tuple-element.152), kind=kLoop, calls=%fused_computation.26 | loop fusion | flops 10485248 | bytes 6474752 | tf_op jit(solution)/shard_map/reduce_sum | solution.py:86
  146.1 0.2 fusion.18
  146.3 5.6 %psum.14 = f32[64,5]{0,1:T(8,128)S(1)} all-reduce(f32[64,5]{0,1:T(8,128)S(1)} %fusion.18), channel_id=1, replica_groups=mesh['dp'=8,'group'=4] {'group'}, use_global_device_ids=true, to_apply=%region_7.9 | all-reduce | flops 320 | bytes 2560 | tf_op jit(solution)/shard_map/psum | solution.py:90
  152.0 20.7 %psum.15 = f32[64,5]{0,1:T(8,128)S(1)} all-reduce(f32[64,5]{0,1:T(8,128)S(1)} %psum.14), channel_id=1, replica_groups=mesh['dp'=8,'group'=4] {'dp'}, use_global_device_ids=true, to_apply=%region_8.10 | all-reduce | flops 320 | bytes 2560 | tf_op jit(solution)/shard_map/psum | solution.py:90
  172.6 0.2 fusion.17
  172.8 0.3 fusion.16
  173.1 0.1 fusion.37
  173.2 4.1 %copy.55 = bf16[256,4096]{1,0:T(8,128)(2,1)} copy(bf16[256,4096]{0,1:T(8,128)(2,1)} %bitcast.79) | data formatting | bytes 4194304 | tf_op jit(solution)/shard_map/reshape | solution.py:44
  177.3 5.9 %select_convert_fusion = (bf16[256,4096]{1,0:T(8,128)(2,1)}, bf16[256,4096]{1,0:T(8,128)(2,1)}) fusion(bf16[256,4096]{1,0:T(8,128)(2,1)} %copy.55, f32[256]{0:T(256)S(1)} %bitcast.89, f32[256]{0:T(256)S(1)} %bitcast.87, s32[256]{0:T(256)S(1)} %fusion.20, f32[256]{0:T(256)S(1)} %bitcast.90, f32[256]{0:T(256)S(1)} %bitcast.88, f32[2,128,4096]{2,1,0:T(8,128)} %copy-done.4), kind=kLoop, calls=%fused_computation.24 | loop fusion | flops 13631488 | bytes 10490880 | tf_op jit(solution)/shard_map/convert_element_type | solution.py:100
  (125 shorter events, 2.3 us)
Async XLA Ops:
  0.6 11.1 %copy-start = (bf16[256,4096]{1,0:T(8,128)(2,1)S(1)}, bf16[256,4096]{1,0:T(8,128)(2,1)}, u32[]{:S(2)}) copy-start(bf16[256,4096]{1,0:T(8,128)(2,1)} %param.11) | copy-start | bytes 6291460
  4.4 17.6 %all-to-all-start = ((f32[8,32,2]{1,2,0:T(2,128)}), f32[8,32,2]{1,2,0:T(2,128)S(1)}, u32[]{:S(2)}, u32[]{:S(2)}) async-start(f32[8,32,2]{1,2,0:T(2,128)} %broadcast_select_fusion.3), calls=%async_computation | async-start | bytes 16384 | tf_op jit(solution)/shard_map/all_to_all | solution.py:107
  22.0 58.4 %copy-start.6 = (s32[2,128]{1,0:T(2,128)S(1)}, s32[2,128]{1,0:T(2,128)}, u32[]{:S(2)}) copy-start(s32[2,128]{1,0:T(2,128)} %param.16) | copy-start | bytes 3076
  76.0 51.6 %all-to-all-start.1 = ((bf16[8,32,4096]{2,1,0:T(8,128)(2,1)}), bf16[8,32,4096]{2,1,0:T(8,128)(2,1)}, u32[]{:S(2)}, u32[]{:S(2)}) async-start(bf16[8,32,4096]{2,1,0:T(8,128)(2,1)} %get-tuple-element.155), calls=%async_computation.1 | async-start | bytes 4194304 | tf_op jit(solution)/shard_map/all_to_all | solution.py:115
  84.5 1.3 copy-start.1
  127.6 3.0 %copy-start.2 = (bf16[2,128,4096]{2,1,0:T(8,128)(2,1)S(1)}, bf16[2,128,4096]{2,1,0:T(8,128)(2,1)}, u32[]{:S(2)}) copy-start(bf16[2,128,4096]{2,1,0:T(8,128)(2,1)} %copy-done.1) | copy-start | bytes 6291460
  127.6 3.5 %copy-start.5 = (f32[256,4095]{1,0:T(8,128)S(1)}, f32[256,4095]{1,0:T(8,128)}, u32[]{:S(2)}) copy-start(f32[256,4095]{1,0:T(8,128)} %slice.58) | copy-start | bytes 12579844
  130.6 2.3 %copy-start.4 = (f32[2,128,4096]{2,1,0:T(8,128)}, f32[2,128,4096]{2,1,0:T(8,128)S(1)}, u32[]{:S(2)}) copy-start(f32[2,128,4096]{2,1,0:T(8,128)S(1)} %get-tuple-element.156) | copy-start | bytes 12582916
  135.7 2.0 %copy-start.3 = (f32[256,32,128]{0,2,1:T(8,128)}, f32[256,32,128]{0,2,1:T(8,128)S(1)}, u32[]{:S(2)}) copy-start(f32[256,32,128]{0,2,1:T(8,128)S(1)} %fusion.14) | copy-start | bytes 12582916
  137.7 8.4 %copy-start.7 = (s32[256]{0:T(256)S(1)}, s32[256]{0:T(256)}, u32[]{:S(2)}) copy-start(s32[256]{0:T(256)} %param.17) | copy-start | bytes 3076
